TPU v7x, 512 devices: a whole 4x8x8 slice. The times are simulated.
512 devices in a mesh: dom: 32 (over z, x), snap: 16 (over y, core).
Axes of the slice: x: 4, y: 8, z: 8, core: 2. Of those that a mesh axis runs over, the one named last changes fastest.
Arguments:
- feat: bfloat16 [16, 4096, 512], P('snap', 'dom'), may hold values from -6 to 6
- w_struct: bfloat16 [512, 1536], replicated, may hold values from -0.25 to 0.25
- w_temp: bfloat16 [512, 1536], replicated, may hold values from -0.25 to 0.25
- pos_embed: bfloat16 [16, 512], replicated, may hold values from -3 to 3
- rel_bias: float32 [4, 8], replicated, may hold values from -1.5 to 1.5
- nbr: int32 [16, 4096, 8], P('snap', 'dom'), may hold values from 0 to 383
- rel_type: int32 [16, 4096, 8], P('snap', 'dom'), may hold values from 0 to 3
- send_idx: int32 [16, 32, 32, 8], P('snap', 'dom'), may hold values from 0 to 127
- active: int32 [16, 4096], P(None, ('dom', 'snap')), may hold values 0 or 1
- cotangent: bfloat16 [16, 4096, 512], P(None, ('dom', 'snap')), may hold values from -6 to 6
Outputs:
- grad_feat: bfloat16 [16, 4096, 512], P('snap', 'dom')
- grad_wtemp: float32 [512, 1536], P('snap')
Inputs may be any that keep to these rules, and one draw needn't show every extreme that they name: `nbr`: rows of the partition's key table: its 128 own entities first, then 8 halo rows from each partition in order.
All inputs are finite; a program needn't handle non-finite values. No bound on the sum of `active` on one device may be relied on, other than what follows from the above.
Results may differ from a plain program's by a relative error of at most 0.024.
Values may be sent and summed in bfloat16 or wider, within the bound.
A program may use at most 64 MiB of HBM per device.

v0:
```python
import jax
import jax.numpy as jnp
from jax import lax
from jax.sharding import PartitionSpec as P

HEADS = 8


def edge_scores(rel_ids, rel_bias):
    onehot = (rel_ids[..., None] == jnp.arange(rel_bias.shape[0], dtype=jnp.int32)).astype(
        jnp.float32
    )
    return jnp.einsum("rek,kh->reh", onehot, rel_bias, precision=lax.Precision.HIGHEST)


def struct_core(query, key_tab, val_tab, links, edge_add):
    row_count, width = query.shape
    slots = links.shape[1]
    head_dim = width // HEADS
    keys_g = key_tab[links].reshape(row_count, slots, HEADS, head_dim)
    vals_g = val_tab[links].reshape(row_count, slots, HEADS, head_dim)
    query_h = query.reshape(row_count, HEADS, head_dim)
    scores = jnp.einsum("rhc,rehc->reh", query_h, keys_g) * head_dim ** (-0.5) + edge_add
    weights = jax.nn.softmax(scores, axis=1)
    rounded = lax.optimization_barrier(weights.astype(jnp.bfloat16)).astype(jnp.float32)
    return jnp.einsum("reh,rehc->rhc", rounded, vals_g).reshape(row_count, width)


def temp_allowed(active_blk):
    snaps = active_blk.shape[0]
    later = jnp.arange(snaps, dtype=jnp.int32)[:, None]
    earlier = jnp.arange(snaps, dtype=jnp.int32)[None, :]
    causal = (earlier <= later)[..., None]
    itself = (earlier == later)[..., None]
    return causal & (itself | (active_blk[None, :, :] == 1))


def temp_core(t_query, t_key, t_value, allowed):
    snaps, count, width = t_query.shape
    head_dim = width // HEADS
    query_h = t_query.reshape(snaps, count, HEADS, head_dim)
    key_h = t_key.reshape(snaps, count, HEADS, head_dim)
    value_h = t_value.reshape(snaps, count, HEADS, head_dim)
    scores = jnp.einsum("tmhc,umhc->tumh", query_h, key_h) * head_dim ** (-0.5)
    scores = jnp.where(allowed[..., None], scores, -1e30)
    weights = jax.nn.softmax(scores, axis=1)
    rounded = lax.optimization_barrier(weights.astype(jnp.bfloat16)).astype(jnp.float32)
    return jnp.einsum("tumh,umhc->tmhc", rounded, value_h).reshape(snaps, count, width)


def per_device(
    feat, w_struct, w_temp, pos_embed, rel_bias, nbr, rel_type, send_idx, active, cotangent
):
    x_rows = feat[0]
    local_count, width = x_rows.shape
    dom_count = lax.axis_size("dom")
    route = send_idx[0, 0]
    halo_per = route.shape[1]
    route_flat = route.reshape(-1)
    projected = jnp.dot(x_rows, w_struct, preferred_element_type=jnp.float32).astype(jnp.bfloat16)
    pair_cols = projected[:, width:]
    tiles = pair_cols[route_flat].reshape(dom_count, halo_per, 2 * width)
    arrived = lax.all_to_all(tiles, "dom", split_axis=0, concat_axis=0, tiled=True).reshape(
        -1, 2 * width
    )
    query_f = projected[:, :width].astype(jnp.float32)
    table = jnp.concatenate([pair_cols, arrived], axis=0).astype(jnp.float32)
    edge_add = edge_scores(rel_type[0], rel_bias)
    links = nbr[0]
    summed = struct_core(query_f, table[:, :width], table[:, width:], links, edge_add)
    hidden = (x_rows.astype(jnp.float32) + jax.nn.elu(summed)).astype(jnp.bfloat16)
    by_entity = lax.all_to_all(hidden[None], "snap", split_axis=1, concat_axis=0, tiled=True)
    snaps = by_entity.shape[0]
    z_in = (by_entity.astype(jnp.float32) + pos_embed.astype(jnp.float32)[:, None, :]).astype(
        jnp.bfloat16
    )
    z_flat = z_in.reshape(-1, width)
    t_proj = jnp.dot(z_flat, w_temp, preferred_element_type=jnp.float32).astype(jnp.bfloat16)
    t_proj = t_proj.reshape(snaps, -1, 3 * width).astype(jnp.float32)
    allowed = temp_allowed(active)
    cot_f = cotangent.astype(jnp.float32)
    _, pull = jax.vjp(
        lambda a_in, b_in, c_in: temp_core(a_in, b_in, c_in, allowed),
        t_proj[..., :width],
        t_proj[..., width : 2 * width],
        t_proj[..., 2 * width :],
    )
    grads_t = pull(cot_f)
    dt_proj = jnp.concatenate(grads_t, axis=-1).astype(jnp.bfloat16).reshape(-1, 3 * width)
    terms = lax.dot_general(
        z_flat, dt_proj, (((0,), (0,)), ((), ())), preferred_element_type=jnp.float32
    )
    share = lax.psum_scatter(terms.astype(jnp.bfloat16), "snap", scatter_dimension=0, tiled=True)
    grad_wtemp = lax.psum(share, "dom").astype(jnp.float32)
    d_z = cot_f + jnp.dot(dt_proj, w_temp.T, preferred_element_type=jnp.float32).reshape(
        snaps, -1, width
    )
    returned = lax.all_to_all(
        d_z.astype(jnp.bfloat16), "snap", split_axis=0, concat_axis=1, tiled=True
    )[0]
    dh_f = returned.astype(jnp.float32)
    d_agg = dh_f * jnp.where(summed > 0, 1.0, jnp.exp(summed))
    _, pull_s = jax.vjp(
        lambda a_in, b_in, c_in: struct_core(a_in, b_in, c_in, links, edge_add),
        query_f,
        table[:, :width],
        table[:, width:],
    )
    d_query, d_key, d_val = pull_s(d_agg)
    halo_back = jnp.concatenate([d_key[local_count:], d_val[local_count:]], axis=-1)
    halo_back = halo_back.reshape(dom_count, halo_per, 2 * width)
    came_back = (
        lax.all_to_all(
            halo_back.astype(jnp.bfloat16), "dom", split_axis=0, concat_axis=0, tiled=True
        )
        .astype(halo_back.dtype)
        .reshape(-1, 2 * width)
    )
    owned = jnp.concatenate([d_key[:local_count], d_val[:local_count]], axis=-1)
    owned = owned.at[route_flat].add(came_back)
    d_proj = jnp.concatenate([d_query, owned], axis=-1).astype(jnp.bfloat16)
    grad_rows = (dh_f + jnp.dot(d_proj, w_struct.T, preferred_element_type=jnp.float32)).astype(
        jnp.bfloat16
    )
    return (grad_rows[None], grad_wtemp)


def solution(mesh):
    return jax.shard_map(
        per_device,
        mesh=mesh,
        in_specs=(
            P("snap", "dom", None),
            P(),
            P(),
            P(),
            P(),
            P("snap", "dom", None),
            P("snap", "dom", None),
            P("snap", "dom", None, None),
            P(None, ("dom", "snap")),
            P(None, ("dom", "snap"), None),
        ),
        out_specs=(P("snap", "dom", None), P("snap", None)),
        check_vma=False,
    )
```

profile of v0, /device:TPU:8, one launch (start us, length us, event | category | flops | bytes accessed | tf_op | source)
XLA Modules:
  0.0 353.8 jit_solution(8830739789273474780)
XLA Ops:
  7.2 0.8 compare_select_fusion.2
  8.2 1.9 convolution_convert_fusion.1
  10.3 2.0 gather_fusion
  12.3 13.3 %all-to-all-start = ((bf16[32,8,1024]{2,1,0:T(8,128)(2,1)}), bf16[32,8,1024]{2,1,0:T(8,128)(2,1)S(1)}, u32[]{:S(2)}, u32[]{:S(2)}) async-start(bf16[32,8,1024]{2,1,0:T(8,128)(2,1)} %bitcast.7), calls=%async_computation | async-start | bytes 1048576 | tf_op jit(solution)/shard_map/all_to_all | solution.py:63
  25.6 0.8 copy.69
  26.7 0.6 broadcast_compare_fusion
  27.3 16.1 %all-to-all-done = bf16[32,8,1024]{2,1,0:T(8,128)(2,1)S(1)} async-done(((bf16[32,8,1024]{2,1,0:T(8,128)(2,1)}), bf16[32,8,1024]{2,1,0:T(8,128)(2,1)S(1)}, u32[]{:S(2)}, u32[]{:S(2)}) %all-to-all-start) | async-done | bytes 524320 | tf_op jit(solution)/shard_map/all_to_all | solution.py:63
  43.3 0.8 copy-done.3
  44.1 1.1 pad_maximum_fusion.1
  45.2 5.1 %gather_fusion.1 = bf16[1024,512]{1,0:T(8,128)(2,1)} fusion(bf16[384,512]{1,0:T(8,128)(2,1)S(1)} %get-tuple-element.3, s32[1024]{0:T(1024)S(1)} %get-tuple-element.20), kind=kCustom, calls=%fused_computation.1 | custom fusion | bytes 2101248 | tf_op jit(solution)/shard_map/gather | solution.py:20
  50.3 3.9 %reshape.244 = bf16[128,8,8,64]{3,2,1,0:T(8,128)(2,1)} reshape(bf16[1024,512]{1,0:T(8,128)(2,1)} %gather_fusion.1) | data formatting | bytes 2097152 | tf_op jit(solution)/shard_map/reshape | solution.py:20
  54.2 3.6 %multiply_reduce_fusion.3 = f32[128,8,8]{1,2,0:T(8,128)} fusion(f32[128,8,64]{2,1,0:T(8,128)S(1)} %copy.120, bf16[128,8,8,64]{3,2,1,0:T(8,128)(2,1)} %reshape.244), kind=kLoop, calls=%fused_computation.10 | loop fusion | flops 1564672 | bytes 1343488
  57.8 1.2 copy.98
  59.3 1.0 copy.121
  60.3 5.1 %gather_fusion.2 = bf16[1024,512]{1,0:T(8,128)(2,1)} fusion(bf16[384,512]{1,0:T(8,128)(2,1)S(1)} %get-tuple-element.2, s32[1024]{0:T(1024)S(1)} %get-tuple-element.20), kind=kCustom, calls=%fused_computation.2 | custom fusion | bytes 2101248 | tf_op jit(solution)/shard_map/gather | solution.py:21
  65.4 4.0 %reshape.246 = bf16[128,8,8,64]{3,2,1,0:T(8,128)(2,1)} reshape(bf16[1024,512]{1,0:T(8,128)(2,1)} %gather_fusion.2) | data formatting | bytes 2097152 | tf_op jit(solution)/shard_map/reshape | solution.py:21
  69.3 2.6 multiply_reduce_fusion.2
  72.2 1.1 fusion.45
  73.4 0.5 broadcast.154
  73.9 1.4 reduce.8
  75.3 0.7 reshape.337
  76.1 7.6 %all-to-all-start.1 = ((bf16[16,2,2048]{2,1,0:T(2,128)(2,1)}), bf16[16,2,2048]{2,1,0:T(2,128)(2,1)S(1)}, u32[]{:S(2)}, u32[]{:S(2)}) async-start(bf16[16,2,2048]{2,1,0:T(2,128)(2,1)} %reshape.337), calls=%async_computation.1 | async-start | bytes 262144 | tf_op jit(solution)/shard_map/all_to_all | solution.py:72
  84.2 6.8 %all-to-all-done.1 = bf16[16,2,2048]{2,1,0:T(2,128)(2,1)S(1)} async-done(((bf16[16,2,2048]{2,1,0:T(2,128)(2,1)}), bf16[16,2,2048]{2,1,0:T(2,128)(2,1)S(1)}, u32[]{:S(2)}, u32[]{:S(2)}) %all-to-all-start.1) | async-done | bytes 131104 | tf_op jit(solution)/shard_map/all_to_all | solution.py:72
  91.2 0.4 fusion.2
  91.5 0.7 fusion.74
  92.3 1.1 reshape.251
  93.4 1.2 reshape.249
  94.6 1.1 fusion.9
  95.7 0.9 reshape.252
  96.6 1.4 fusion.8
  98.0 2.1 fusion.76
  100.3 0.6 neg.12
  100.9 2.3 fusion.10
  103.2 2.2 fusion.11
  105.4 1.1 copy.82
  106.5 0.9 concatenate.27
  107.4 1.6 constant_dynamic-update-slice_fusion.2
  109.0 1.0 copy.84
  110.0 0.9 concatenate.28
  111.4 1.6 constant_dynamic-update-slice_fusion.1
  113.0 0.7 constant_dynamic-update-slice_fusion
  113.7 2.9 fusion.1
  116.6 1.3 fusion.17
  117.9 4.7 %all-to-all-start.2 = ((bf16[16,8,512]{2,1,0:T(8,128)(2,1)}), bf16[16,8,512]{2,1,0:T(8,128)(2,1)S(1)}, u32[]{:S(2)}, u32[]{:S(2)}) async-start(bf16[16,8,512]{2,1,0:T(8,128)(2,1)} %fusion.17), calls=%async_computation.2 | async-start | bytes 262144 | tf_op jit(solution)/shard_map/all_to_all | solution.py:98
  122.6 1.0 copy.90
  123.6 6.6 %all-to-all-done.2 = bf16[16,8,512]{2,1,0:T(8,128)(2,1)S(1)} async-done(((bf16[16,8,512]{2,1,0:T(8,128)(2,1)}), bf16[16,8,512]{2,1,0:T(8,128)(2,1)S(1)}, u32[]{:S(2)}, u32[]{:S(2)}) %all-to-all-start.2) | async-done | bytes 131104 | tf_op jit(solution)/shard_map/all_to_all | solution.py:98
  130.9 5.6 %multiply_reduce_fusion.1 = (bf16[128,8,8]{1,2,0:T(8,128)(2,1)S(1)}, f32[128,8,8,64]{3,2,1,0:T(8,128)}) fusion(f32[128,8,64]{2,1,0:T(8,128)S(1)} %copy.122, bf16[128,8,8,64]{3,2,1,0:T(8,128)(2,1)} %reshape.246, f32[128,8,8]{1,2,0:T(8,128)} %copy.90), kind=kLoop, calls=%fused_computation.8 | loop fusion | flops 2088960 | bytes 3457024
  136.5 4.8 %reshape.300 = f32[1024,512]{1,0:T(8,128)} reshape(f32[128,8,8,64]{3,2,1,0:T(8,128)} %get-tuple-element.7) | data formatting | bytes 4194304 | tf_op jit(solution)/shard_map/transpose(jvp())/reshape | solution.py:21
  141.7 5.6 %multiply_reduce_fusion = (bf16[128,8,64]{2,1,0:T(8,128)(2,1)}, f32[128,8,8,64]{3,2,1,0:T(8,128)}) fusion(f32[128,8,8]{1,2,0:T(8,128)S(1)} %copy.123, bf16[128,8,8,64]{3,2,1,0:T(8,128)(2,1)} %reshape.244, f32[128,8,64]{2,1,0:T(8,128)S(1)} %copy.120), kind=kLoop, calls=%fused_computation.7 | loop fusion | flops 2031616 | bytes 3571712
  147.4 4.8 %reshape.292 = f32[1024,512]{1,0:T(8,128)} reshape(f32[128,8,8,64]{3,2,1,0:T(8,128)} %get-tuple-element.5) | data formatting | bytes 4194304 | tf_op jit(solution)/shard_map/transpose(jvp())/reshape | solution.py:20
  152.2 7.5 %scatter_custom_fusion.1 = f32[384,512]{1,0:T(8,128)S(1)} fusion(s32[1024]{0:T(1024)S(1)} %reshape.274, f32[1024,512]{1,0:T(8,128)} %reshape.300, f32[]{:T(128)} %constant.15.clone.1), kind=kCustom, calls=%fused_computation.65 | custom fusion | flops 524288 | bytes 786944 | tf_op jit(solution)/shard_map/transpose(jvp())/scatter-add | solution.py:21
  159.7 7.5 %scatter_custom_fusion = f32[384,512]{1,0:T(8,128)S(1)} fusion(s32[1024]{0:T(1024)S(1)} %reshape.274, f32[1024,512]{1,0:T(8,128)} %reshape.292, f32[]{:T(128)} %constant.15.clone.1), kind=kCustom, calls=%fused_computation.67 | custom fusion | flops 524288 | bytes 786944 | tf_op jit(solution)/shard_map/transpose(jvp())/scatter-add | solution.py:20
  167.2 1.0 maximum_bitcast_fusion
  168.2 4.6 %all-to-all-start.3 = ((bf16[32,8,1024]{2,1,0:T(8,128)(2,1)}), bf16[32,8,1024]{2,1,0:T(8,128)(2,1)}, u32[]{:S(2)}, u32[]{:S(2)}) async-start(bf16[32,8,1024]{2,1,0:T(8,128)(2,1)} %maximum_bitcast_fusion), calls=%async_computation.3 | async-start | bytes 1048576 | tf_op jit(solution)/shard_map/all_to_all | solution.py:113
  173.2 1.8 slice.61
  175.0 1.8 copy.119
  176.8 1.7 copy.91
  178.4 1.8 pad_maximum_fusion
  180.2 10.9 %all-to-all-done.3 = bf16[32,8,1024]{2,1,0:T(8,128)(2,1)} async-done(((bf16[32,8,1024]{2,1,0:T(8,128)(2,1)}), bf16[32,8,1024]{2,1,0:T(8,128)(2,1)}, u32[]{:S(2)}, u32[]{:S(2)}) %all-to-all-start.3) | async-done | bytes 524320 | tf_op jit(solution)/shard_map/all_to_all | solution.py:113
  191.1 5.0 %scatter_custom_fusion.2 = f32[128,1024]{1,0:T(8,128)} fusion(f32[128,1024]{1,0:T(8,128)} %pad_maximum_fusion, s32[256]{0:T(256)S(1)} %bitcast.139, bf16[32,8,1024]{2,1,0:T(8,128)(2,1)} %all-to-all-done.3), kind=kCustom, calls=%fused_computation.39 | custom fusion | flops 524288 | bytes 1048576 | tf_op jit(solution)/shard_map/scatter-add | solution.py:120
  196.1 1.1 convert.51
  197.3 2.2 fusion.20
  199.5 145.9 %all-reduce.2.cloned.1.call-done = bf16[32,1536]{1,0:T(8,128)(2,1)} async-done(((bf16[32,1536]{1,0:T(8,128)(2,1)}), bf16[32,1536]{1,0:T(8,128)(2,1)}) %all-reduce.2.cloned.1.call-update) | async-done | bytes 98320 | tf_op jit(solution)/shard_map/psum | solution.py:94
  345.4 1.6 convert_element_type.131
  (84 shorter events, 4.4 us)
Async XLA Ops:
  7.2 84.0 %copy-start = (bf16[512,1536]{1,0:T(8,128)(2,1)S(1)}, bf16[512,1536]{1,0:T(8,128)(2,1)}, u32[]{:S(2)}) copy-start(bf16[512,1536]{1,0:T(8,128)(2,1)} %param.12) | copy-start | bytes 4718596
  7.2 2.9 copy-start.15
  10.3 15.3 %copy-start.12 = (bf16[1,128,512]{2,1,0:T(8,128)(2,1)S(1)}, bf16[1,128,512]{2,1,0:T(8,128)(2,1)}, u32[]{:S(2)}) copy-start(bf16[1,128,512]{2,1,0:T(8,128)(2,1)} %param.10) | copy-start | bytes 393220
  12.3 14.4 %copy-start.17 = (s32[16,8]{0,1:T(8,128)S(1)}, s32[16,8]{0,1:T(8,128)}, u32[]{:S(2)}) copy-start(s32[16,8]{0,1:T(8,128)} %param.18) | copy-start | bytes 1540
  12.3 31.1 %all-to-all-start = ((bf16[32,8,1024]{2,1,0:T(8,128)(2,1)}), bf16[32,8,1024]{2,1,0:T(8,128)(2,1)S(1)}, u32[]{:S(2)}, u32[]{:S(2)}) async-start(bf16[32,8,1024]{2,1,0:T(8,128)(2,1)} %bitcast.7), calls=%async_computation | async-start | bytes 1048576 | tf_op jit(solution)/shard_map/all_to_all | solution.py:63
  43.3 0.8 copy-start.3
  54.2 4.8 %copy-start.16 = (s32[1,128,8]{1,2,0:T(8,128)S(1)}, s32[1,128,8]{1,2,0:T(8,128)}, u32[]{:S(2)}) copy-start(s32[1,128,8]{1,2,0:T(8,128)} %param.16) | copy-start | bytes 12292
  54.2 4.8 %copy-start.19 = (f32[4,8]{1,0:T(4,128)S(1)}, f32[4,8]{1,0:T(4,128)}, u32[]{:S(2)}) copy-start(f32[4,8]{1,0:T(4,128)} %param.14) | copy-start | bytes 388
  65.4 4.0 %copy-start.4 = (f32[128,8,8]{1,2,0:T(8,128)S(1)}, f32[128,8,8]{1,2,0:T(8,128)}, u32[]{:S(2)}) copy-start(f32[128,8,8]{1,2,0:T(8,128)} %copy.121) | copy-start | bytes 98308
  71.9 11.9 %copy-start.14 = (bf16[16,512]{1,0:T(8,128)(2,1)S(1)}, bf16[16,512]{1,0:T(8,128)(2,1)}, u32[]{:S(2)}) copy-start(bf16[16,512]{1,0:T(8,128)(2,1)} %param.13) | copy-start | bytes 49156
  71.9 11.9 %copy-start.10 = (bf16[16,8,512]{2,1,0:T(8,128)(2,1)S(1)}, bf16[16,8,512]{2,1,0:T(8,128)(2,1)}, u32[]{:S(2)}) copy-start(bf16[16,8,512]{2,1,0:T(8,128)(2,1)} %param.19) | copy-start | bytes 393220
  71.9 12.1 %copy-start.18 = (pred[16,8]{0,1:T(8,128)(4,1)S(1)}, pred[16,8]{0,1:T(8,128)(4,1)}, u32[]{:S(2)}) copy-start(pred[16,8]{0,1:T(8,128)(4,1)} %broadcast_compare_fusion) | copy-start | bytes 388
  76.1 14.9 %all-to-all-start.1 = ((bf16[16,2,2048]{2,1,0:T(2,128)(2,1)}), bf16[16,2,2048]{2,1,0:T(2,128)(2,1)S(1)}, u32[]{:S(2)}, u32[]{:S(2)}) async-start(bf16[16,2,2048]{2,1,0:T(2,128)(2,1)} %reshape.337), calls=%async_computation.1 | async-start | bytes 262144 | tf_op jit(solution)/shard_map/all_to_all | solution.py:72
  83.6 113.6 %reduce-scatter.2.cloned.1.call-start = ((), (), s32[]{:S(2)}) async-start(), calls=%async_computation.5 | async-start | bytes 1671168 | tf_op jit(solution)/shard_map/reduce_scatter | solution.py:93
  84.2 12.4 %copy-start.13 = (pred[16,16,8]{0,1,2:T(8,128)(4,1)}, pred[16,16,8]{0,1,2:T(8,128)(4,1)S(1)}, u32[]{:S(2)}) copy-start(pred[16,16,8]{0,1,2:T(8,128)(4,1)S(1)} %or_and_fusion) | copy-start | bytes 6148
  91.1 1.1 copy-start.8
  93.4 6.7 %copy-start.6 = (bf16[16,8,8,64]{3,2,1,0:T(8,128)(2,1)}, bf16[16,8,8,64]{3,2,1,0:T(8,128)(2,1)S(1)}, u32[]{:S(2)}) copy-start(bf16[16,8,8,64]{3,2,1,0:T(8,128)(2,1)S(1)} %reshape.251) | copy-start | bytes 393220
  96.6 3.5 copy-start.5
  105.4 8.2 %copy-start.9 = (bf16[128,1,512]{2,1,0:T(2,128)(2,1)S(1)}, bf16[128,1,512]{2,1,0:T(2,128)(2,1)}, u32[]{:S(2)}) copy-start(bf16[128,1,512]{2,1,0:T(2,128)(2,1)} %copy-done.8) | copy-start | bytes 393220
  113.7 2.9 copy-start.7
  113.7 3.0 copy-start.11
  117.9 12.2 %all-to-all-start.2 = ((bf16[16,8,512]{2,1,0:T(8,128)(2,1)}), bf16[16,8,512]{2,1,0:T(8,128)(2,1)S(1)}, u32[]{:S(2)}, u32[]{:S(2)}) async-start(bf16[16,8,512]{2,1,0:T(8,128)(2,1)} %fusion.17), calls=%async_computation.2 | async-start | bytes 262144 | tf_op jit(solution)/shard_map/all_to_all | solution.py:98
  167.1 6.0 %copy-start.2 = (f32[384,512]{1,0:T(8,128)}, f32[384,512]{1,0:T(8,128)S(1)}, u32[]{:S(2)}) copy-start(f32[384,512]{1,0:T(8,128)S(1)} %scatter_custom_fusion) | copy-start | bytes 2359300
  168.2 22.9 %all-to-all-start.3 = ((bf16[32,8,1024]{2,1,0:T(8,128)(2,1)}), bf16[32,8,1024]{2,1,0:T(8,128)(2,1)}, u32[]{:S(2)}, u32[]{:S(2)}) async-start(bf16[32,8,1024]{2,1,0:T(8,128)(2,1)} %maximum_bitcast_fusion), calls=%async_computation.3 | async-start | bytes 1048576 | tf_op jit(solution)/shard_map/all_to_all | solution.py:113
  172.8 172.5 %all-reduce.2.cloned.1.call-start = ((), (), s32[]{:S(2)}) async-start(), calls=%async_computation.6 | async-start | bytes 196608 | tf_op jit(solution)/shard_map/psum | solution.py:94
  173.2 24.1 %copy-start.1 = (bf16[512,1536]{1,0:T(8,128)(2,1)S(1)}, bf16[512,1536]{1,0:T(8,128)(2,1)}, u32[]{:S(2)}) copy-start(bf16[512,1536]{1,0:T(8,128)(2,1)} %param.11) | copy-start | bytes 4718596
Sparse Core Ops, SparseCore 0:
  116.7 52.3 reduce-scatter.1
  197.4 147.9 all-reduce.1
where the time goes:
time: 355 us; the launch traced here: 354 us
  waiting for transfers between devices  186 us (52%)
  local copies, waits for them, and re-layouts  55.2 us (16%)
  other arithmetic  50.8 us (14%)
  starting transfers between devices  30.7 us (9%)
  matrix products  16.1 us (5%)
  between operations  14.6 us (4%)
    psum x1, waiting for transfers between devices, per_device(): grad_wtemp = lax.psum(share, 'dom').astype(jnp.float32)  146 us
    unnamed x5, other arithmetic  18.8 us
    all_to_all x1, waiting for transfers between devices, per_device(): lax.all_to_all(tiles, 'dom', split_axis=0, concat_axis=0, tiled=True)  16.1 us
    all_to_all x1, starting transfers between devices, per_device(): lax.all_to_all(tiles, 'dom', split_axis=0, concat_axis=0, tiled=True)  13.3 us
    all_to_all x1, waiting for transfers between devices, per_device(): lax.all_to_all(halo_back.astype(jnp.bfloat16), 'dom', split_axis=0, conca...  10.9 us
    reshape x2, local copies, waits for them, and re-layouts, struct_core(): vals_g = val_tab[links].reshape(row_count, slots, HEADS, head_dim)  8.76 us
    reshape x2, local copies, waits for them, and re-layouts, struct_core(): keys_g = key_tab[links].reshape(row_count, slots, HEADS, head_dim)  8.71 us
    unnamed x51, local copies, waits for them, and re-layouts  7.9 us
  transfers between devices with their start and end apart: 6, of which 5 were waited for; matrix products, arithmetic and copies ran while one was open for 16% of the time, Pallas kernels for 0%

commit v1 on v0

--- a/solution.py
+++ b/solution.py
@@ -91,7 +91,7 @@
         z_flat, dt_proj, (((0,), (0,)), ((), ())), preferred_element_type=jnp.float32
     )
     share = lax.psum_scatter(terms.astype(jnp.bfloat16), "snap", scatter_dimension=0, tiled=True)
-    grad_wtemp = lax.psum(share, "dom").astype(jnp.float32)
+    grad_wtemp = jnp.sum(lax.all_gather(share, "dom"), axis=0).astype(jnp.float32)
     d_z = cot_f + jnp.dot(dt_proj, w_temp.T, preferred_element_type=jnp.float32).reshape(
         snaps, -1, width
     )

time: 355 us -> 278 us (0.78)
  the two profiles are of different devices: /device:TPU:8 before, /device:TPU:1 now
where the time goes in v1:
time: 278 us; the launch traced here: 277 us
  waiting for transfers between devices  97.5 us (35%)
  local copies, waits for them, and re-layouts  55.4 us (20%)
  other arithmetic  52.2 us (19%)
  starting transfers between devices  40.7 us (15%)
  matrix products  16.1 us (6%)
  between operations  14.6 us (5%)
    reduce_scatter x1, waiting for transfers between devices, per_device(): lax.psum_scatter(terms.astype(jnp.bfloat16), 'snap', scatter_dimension=0,...  51 us
    unnamed x5, other arithmetic  18.8 us
    all_to_all x1, waiting for transfers between devices, per_device(): lax.all_to_all(halo_back.astype(jnp.bfloat16), 'dom', split_axis=0, conca...  15.7 us
    all_to_all x1, waiting for transfers between devices, per_device(): lax.all_to_all(tiles, 'dom', split_axis=0, concat_axis=0, tiled=True)  14.6 us
    all_to_all x1, starting transfers between devices, per_device(): lax.all_to_all(tiles, 'dom', split_axis=0, concat_axis=0, tiled=True)  13.8 us
    all_to_all x1, starting transfers between devices, per_device(): lax.all_to_all(halo_back.astype(jnp.bfloat16), 'dom', split_axis=0, conca...  10.3 us
    all_to_all x1, starting transfers between devices, per_device(): lax.all_to_all(hidden[None], 'snap', split_axis=1, concat_axis=0, tiled=T...  9.54 us
    reshape x2, local copies, waits for them, and re-layouts, struct_core(): keys_g = key_tab[links].reshape(row_count, slots, HEADS, head_dim)  8.84 us
  transfers between devices with their start and end apart: 6, of which 5 were waited for; matrix products, arithmetic and copies ran while one was open for 21% of the time, Pallas kernels for 0%

profile of v1, /device:TPU:1, one launch (start us, length us, event | category | flops | bytes accessed | tf_op | source)
XLA Modules:
  0.0 276.5 jit_solution(5463996496252345527)
XLA Ops:
  7.2 0.8 compare_select_fusion.2
  8.2 1.9 convolution_convert_fusion.1
  10.3 2.0 gather_fusion
  12.3 13.8 %all-to-all-start = ((bf16[32,8,1024]{2,1,0:T(8,128)(2,1)}), bf16[32,8,1024]{2,1,0:T(8,128)(2,1)S(1)}, u32[]{:S(2)}, u32[]{:S(2)}) async-start(bf16[32,8,1024]{2,1,0:T(8,128)(2,1)} %bitcast.7), calls=%async_computation | async-start | bytes 1048576 | tf_op jit(solution)/shard_map/all_to_all | solution.py:63
  26.1 0.8 copy.69
  27.2 0.6 broadcast_compare_fusion
  27.8 14.6 %all-to-all-done = bf16[32,8,1024]{2,1,0:T(8,128)(2,1)S(1)} async-done(((bf16[32,8,1024]{2,1,0:T(8,128)(2,1)}), bf16[32,8,1024]{2,1,0:T(8,128)(2,1)S(1)}, u32[]{:S(2)}, u32[]{:S(2)}) %all-to-all-start) | async-done | bytes 524320 | tf_op jit(solution)/shard_map/all_to_all | solution.py:63
  42.4 0.8 copy-done.3
  43.2 1.1 pad_maximum_fusion.1
  44.3 5.1 %gather_fusion.1 = bf16[1024,512]{1,0:T(8,128)(2,1)} fusion(bf16[384,512]{1,0:T(8,128)(2,1)S(1)} %get-tuple-element.3, s32[1024]{0:T(1024)S(1)} %get-tuple-element.20), kind=kCustom, calls=%fused_computation.1 | custom fusion | bytes 2101248 | tf_op jit(solution)/shard_map/gather | solution.py:20
  49.3 4.0 %reshape.244 = bf16[128,8,8,64]{3,2,1,0:T(8,128)(2,1)} reshape(bf16[1024,512]{1,0:T(8,128)(2,1)} %gather_fusion.1) | data formatting | bytes 2097152 | tf_op jit(solution)/shard_map/reshape | solution.py:20
  53.3 3.6 %multiply_reduce_fusion.3 = f32[128,8,8]{1,2,0:T(8,128)} fusion(f32[128,8,64]{2,1,0:T(8,128)S(1)} %copy.120, bf16[128,8,8,64]{3,2,1,0:T(8,128)(2,1)} %reshape.244), kind=kLoop, calls=%fused_computation.10 | loop fusion | flops 1564672 | bytes 1343488
  56.9 1.2 copy.98
  58.4 1.0 copy.121
  59.4 5.1 %gather_fusion.2 = bf16[1024,512]{1,0:T(8,128)(2,1)} fusion(bf16[384,512]{1,0:T(8,128)(2,1)S(1)} %get-tuple-element.2, s32[1024]{0:T(1024)S(1)} %get-tuple-element.20), kind=kCustom, calls=%fused_computation.2 | custom fusion | bytes 2101248 | tf_op jit(solution)/shard_map/gather | solution.py:21
  64.5 4.0 %reshape.246 = bf16[128,8,8,64]{3,2,1,0:T(8,128)(2,1)} reshape(bf16[1024,512]{1,0:T(8,128)(2,1)} %gather_fusion.2) | data formatting | bytes 2097152 | tf_op jit(solution)/shard_map/reshape | solution.py:21
  68.5 2.6 multiply_reduce_fusion.2
  71.3 1.1 fusion.45
  72.6 0.5 broadcast.154
  73.1 1.4 reduce.9
  74.5 0.7 reshape.338
  75.2 9.5 %all-to-all-start.1 = ((bf16[16,2,2048]{2,1,0:T(2,128)(2,1)}), bf16[16,2,2048]{2,1,0:T(2,128)(2,1)S(1)}, u32[]{:S(2)}, u32[]{:S(2)}) async-start(bf16[16,2,2048]{2,1,0:T(2,128)(2,1)} %reshape.338), calls=%async_computation.1 | async-start | bytes 262144 | tf_op jit(solution)/shard_map/all_to_all | solution.py:72
  85.3 8.3 %all-to-all-done.1 = bf16[16,2,2048]{2,1,0:T(2,128)(2,1)S(1)} async-done(((bf16[16,2,2048]{2,1,0:T(2,128)(2,1)}), bf16[16,2,2048]{2,1,0:T(2,128)(2,1)S(1)}, u32[]{:S(2)}, u32[]{:S(2)}) %all-to-all-start.1) | async-done | bytes 131104 | tf_op jit(solution)/shard_map/all_to_all | solution.py:72
  94.2 0.7 fusion.74
  94.9 1.1 reshape.251
  96.0 1.2 reshape.249
  97.2 1.1 fusion.9
  98.3 0.9 reshape.252
  99.2 1.4 fusion.8
  100.6 2.1 fusion.76
  103.0 0.6 neg.12
  103.6 2.3 fusion.10
  105.9 2.2 fusion.11
  108.1 1.1 copy.82
  109.2 0.9 concatenate.27
  110.1 1.6 constant_dynamic-update-slice_fusion.2
  111.6 1.0 copy.84
  112.6 0.9 concatenate.28
  114.1 1.6 constant_dynamic-update-slice_fusion.1
  115.7 0.7 constant_dynamic-update-slice_fusion
  116.4 2.8 %fusion.1 = bf16[512,1536]{1,0:T(8,128)(2,1)} fusion(bf16[16,8,1536]{2,1,0:T(8,128)(2,1)} %constant_dynamic-update-slice_fusion, f32[16,512]{1,0:T(8,128)S(1)} %convert_element_type.112, bf16[1,128,512]{2,0,1:T(2,128)(2,1)S(1)} %bitcast.134), kind=kOutput, calls=%fused_computation.14 | convolution fusion | flops 202309632 | bytes 2129920 | tf_op jit(solution)/shard_map/dot_general | solution.py:90
  119.3 51.0 %reduce-scatter.2.cloned.1.call-done = bf16[32,1536]{1,0:T(8,128)(2,1)} async-done(((bf16[512,1536]{1,0:T(8,128)(2,1)}), bf16[32,1536]{1,0:T(8,128)(2,1)}) %reduce-scatter.2.cloned.1.call-update) | async-done | bytes 98320 | tf_op jit(solution)/shard_map/reduce_scatter | solution.py:93
  170.3 1.3 fusion.17
  171.7 6.8 %all-to-all-start.2 = ((bf16[16,8,512]{2,1,0:T(8,128)(2,1)}), bf16[16,8,512]{2,1,0:T(8,128)(2,1)S(1)}, u32[]{:S(2)}, u32[]{:S(2)}) async-start(bf16[16,8,512]{2,1,0:T(8,128)(2,1)} %fusion.17), calls=%async_computation.2 | async-start | bytes 262144 | tf_op jit(solution)/shard_map/all_to_all | solution.py:98
  178.4 1.0 copy.90
  179.4 7.9 %all-to-all-done.2 = bf16[16,8,512]{2,1,0:T(8,128)(2,1)S(1)} async-done(((bf16[16,8,512]{2,1,0:T(8,128)(2,1)}), bf16[16,8,512]{2,1,0:T(8,128)(2,1)S(1)}, u32[]{:S(2)}, u32[]{:S(2)}) %all-to-all-start.2) | async-done | bytes 131104 | tf_op jit(solution)/shard_map/all_to_all | solution.py:98
  188.0 5.6 %multiply_reduce_fusion.1 = (bf16[128,8,8]{1,2,0:T(8,128)(2,1)S(1)}, f32[128,8,8,64]{3,2,1,0:T(8,128)}) fusion(f32[128,8,64]{2,1,0:T(8,128)S(1)} %copy.122, bf16[128,8,8,64]{3,2,1,0:T(8,128)(2,1)} %reshape.246, f32[128,8,8]{1,2,0:T(8,128)} %copy.90), kind=kLoop, calls=%fused_computation.8 | loop fusion | flops 2088960 | bytes 3457024
  193.6 4.8 %reshape.300 = f32[1024,512]{1,0:T(8,128)} reshape(f32[128,8,8,64]{3,2,1,0:T(8,128)} %get-tuple-element.7) | data formatting | bytes 4194304 | tf_op jit(solution)/shard_map/transpose(jvp())/reshape | solution.py:21
  198.9 5.6 %multiply_reduce_fusion = (bf16[128,8,64]{2,1,0:T(8,128)(2,1)}, f32[128,8,8,64]{3,2,1,0:T(8,128)}) fusion(f32[128,8,8]{1,2,0:T(8,128)S(1)} %copy.123, bf16[128,8,8,64]{3,2,1,0:T(8,128)(2,1)} %reshape.244, f32[128,8,64]{2,1,0:T(8,128)S(1)} %copy.120), kind=kLoop, calls=%fused_computation.7 | loop fusion | flops 2031616 | bytes 3571712
  204.5 4.9 %reshape.292 = f32[1024,512]{1,0:T(8,128)} reshape(f32[128,8,8,64]{3,2,1,0:T(8,128)} %get-tuple-element.5) | data formatting | bytes 4194304 | tf_op jit(solution)/shard_map/transpose(jvp())/reshape | solution.py:20
  209.4 7.4 %scatter_custom_fusion.1 = f32[384,512]{1,0:T(8,128)S(1)} fusion(s32[1024]{0:T(1024)S(1)} %reshape.274, f32[1024,512]{1,0:T(8,128)} %reshape.300, f32[]{:T(128)} %constant.16.clone.1), kind=kCustom, calls=%fused_computation.65 | custom fusion | flops 524288 | bytes 786944 | tf_op jit(solution)/shard_map/transpose(jvp())/scatter-add | solution.py:21
  216.8 7.5 %scatter_custom_fusion = f32[384,512]{1,0:T(8,128)S(1)} fusion(s32[1024]{0:T(1024)S(1)} %reshape.274, f32[1024,512]{1,0:T(8,128)} %reshape.292, f32[]{:T(128)} %constant.16.clone.1), kind=kCustom, calls=%fused_computation.67 | custom fusion | flops 524288 | bytes 786944 | tf_op jit(solution)/shard_map/transpose(jvp())/scatter-add | solution.py:20
  224.4 1.0 maximum_bitcast_fusion
  225.4 10.3 %all-to-all-start.3 = ((bf16[32,8,1024]{2,1,0:T(8,128)(2,1)}), bf16[32,8,1024]{2,1,0:T(8,128)(2,1)}, u32[]{:S(2)}, u32[]{:S(2)}) async-start(bf16[32,8,1024]{2,1,0:T(8,128)(2,1)} %maximum_bitcast_fusion), calls=%async_computation.3 | async-start | bytes 1048576 | tf_op jit(solution)/shard_map/all_to_all | solution.py:113
  235.7 1.8 slice.61
  237.5 1.8 copy.119
  239.3 1.7 copy.91
  240.9 1.8 pad_maximum_fusion
  242.7 15.7 %all-to-all-done.3 = bf16[32,8,1024]{2,1,0:T(8,128)(2,1)} async-done(((bf16[32,8,1024]{2,1,0:T(8,128)(2,1)}), bf16[32,8,1024]{2,1,0:T(8,128)(2,1)}, u32[]{:S(2)}, u32[]{:S(2)}) %all-to-all-start.3) | async-done | bytes 524320 | tf_op jit(solution)/shard_map/all_to_all | solution.py:113
  258.4 5.0 %scatter_custom_fusion.2 = f32[128,1024]{1,0:T(8,128)} fusion(f32[128,1024]{1,0:T(8,128)} %pad_maximum_fusion, s32[256]{0:T(256)S(1)} %bitcast.141, bf16[32,8,1024]{2,1,0:T(8,128)(2,1)} %all-to-all-done.3), kind=kCustom, calls=%fused_computation.39 | custom fusion | flops 524288 | bytes 1048576 | tf_op jit(solution)/shard_map/scatter-add | solution.py:120
  263.3 1.1 convert.52
  264.4 2.2 fusion.20
  266.6 2.3 reduce_sum.64
  269.0 0.7 convert_element_type.133
  (85 shorter events, 4.5 us)
Async XLA Ops:
  7.2 86.6 %copy-start = (bf16[512,1536]{1,0:T(8,128)(2,1)S(1)}, bf16[512,1536]{1,0:T(8,128)(2,1)}, u32[]{:S(2)}) copy-start(bf16[512,1536]{1,0:T(8,128)(2,1)} %param.12) | copy-start | bytes 4718596
  7.2 2.9 %copy-start.15 = (s32[1,1,32,8]{2,3,1,0:T(8,128)S(1)}, s32[1,1,32,8]{2,3,1,0:T(8,128)}, u32[]{:S(2)}) copy-start(s32[1,1,32,8]{2,3,1,0:T(8,128)} %param.17) | copy-start | bytes 3076
  10.3 15.8 %copy-start.12 = (bf16[1,128,512]{2,1,0:T(8,128)(2,1)S(1)}, bf16[1,128,512]{2,1,0:T(8,128)(2,1)}, u32[]{:S(2)}) copy-start(bf16[1,128,512]{2,1,0:T(8,128)(2,1)} %param.10) | copy-start | bytes 393220
  12.3 15.0 %copy-start.17 = (s32[16,8]{0,1:T(8,128)S(1)}, s32[16,8]{0,1:T(8,128)}, u32[]{:S(2)}) copy-start(s32[16,8]{0,1:T(8,128)} %param.18) | copy-start | bytes 1540
  12.3 30.1 %all-to-all-start = ((bf16[32,8,1024]{2,1,0:T(8,128)(2,1)}), bf16[32,8,1024]{2,1,0:T(8,128)(2,1)S(1)}, u32[]{:S(2)}, u32[]{:S(2)}) async-start(bf16[32,8,1024]{2,1,0:T(8,128)(2,1)} %bitcast.7), calls=%async_computation | async-start | bytes 1048576 | tf_op jit(solution)/shard_map/all_to_all | solution.py:63
  42.4 0.8 copy-start.3
  53.3 4.8 %copy-start.16 = (s32[1,128,8]{1,2,0:T(8,128)S(1)}, s32[1,128,8]{1,2,0:T(8,128)}, u32[]{:S(2)}) copy-start(s32[1,128,8]{1,2,0:T(8,128)} %param.16) | copy-start | bytes 12292
  53.3 4.8 %copy-start.19 = (f32[4,8]{1,0:T(4,128)S(1)}, f32[4,8]{1,0:T(4,128)}, u32[]{:S(2)}) copy-start(f32[4,8]{1,0:T(4,128)} %param.14) | copy-start | bytes 388
  64.5 4.0 %copy-start.4 = (f32[128,8,8]{1,2,0:T(8,128)S(1)}, f32[128,8,8]{1,2,0:T(8,128)}, u32[]{:S(2)}) copy-start(f32[128,8,8]{1,2,0:T(8,128)} %copy.121) | copy-start | bytes 98308
  71.1 13.9 %copy-start.14 = (bf16[16,512]{1,0:T(8,128)(2,1)S(1)}, bf16[16,512]{1,0:T(8,128)(2,1)}, u32[]{:S(2)}) copy-start(bf16[16,512]{1,0:T(8,128)(2,1)} %param.13) | copy-start | bytes 49156
  71.1 13.9 %copy-start.10 = (bf16[16,8,512]{2,1,0:T(8,128)(2,1)S(1)}, bf16[16,8,512]{2,1,0:T(8,128)(2,1)}, u32[]{:S(2)}) copy-start(bf16[16,8,512]{2,1,0:T(8,128)(2,1)} %param.19) | copy-start | bytes 393220
  71.1 14.1 %copy-start.18 = (pred[16,8]{0,1:T(8,128)(4,1)S(1)}, pred[16,8]{0,1:T(8,128)(4,1)}, u32[]{:S(2)}) copy-start(pred[16,8]{0,1:T(8,128)(4,1)} %broadcast_compare_fusion) | copy-start | bytes 388
  75.2 18.4 %all-to-all-start.1 = ((bf16[16,2,2048]{2,1,0:T(2,128)(2,1)}), bf16[16,2,2048]{2,1,0:T(2,128)(2,1)S(1)}, u32[]{:S(2)}, u32[]{:S(2)}) async-start(bf16[16,2,2048]{2,1,0:T(2,128)(2,1)} %reshape.338), calls=%async_computation.1 | async-start | bytes 262144 | tf_op jit(solution)/shard_map/all_to_all | solution.py:72
  84.7 85.6 %reduce-scatter.2.cloned.1.call-start = ((), (), s32[]{:S(2)}) async-start(), calls=%async_computation.5 | async-start | bytes 1671168 | tf_op jit(solution)/shard_map/reduce_scatter | solution.py:93
  85.3 13.9 %copy-start.13 = (pred[16,16,8]{0,1,2:T(8,128)(4,1)}, pred[16,16,8]{0,1,2:T(8,128)(4,1)S(1)}, u32[]{:S(2)}) copy-start(pred[16,16,8]{0,1,2:T(8,128)(4,1)S(1)} %or_and_fusion) | copy-start | bytes 6148
  93.8 1.2 copy-start.8
  96.0 6.7 %copy-start.6 = (bf16[16,8,8,64]{3,2,1,0:T(8,128)(2,1)}, bf16[16,8,8,64]{3,2,1,0:T(8,128)(2,1)S(1)}, u32[]{:S(2)}) copy-start(bf16[16,8,8,64]{3,2,1,0:T(8,128)(2,1)S(1)} %reshape.251) | copy-start | bytes 393220
  99.2 3.5 %copy-start.5 = (bf16[16,16,8,8]{0,1,3,2:T(8,128)(2,1)S(1)}, bf16[16,16,8,8]{0,1,3,2:T(8,128)(2,1)}, u32[]{:S(2)}) copy-start(bf16[16,16,8,8]{0,1,3,2:T(8,128)(2,1)} %fusion.9) | copy-start | bytes 98308
  108.1 8.2 %copy-start.9 = (bf16[128,1,512]{2,1,0:T(2,128)(2,1)S(1)}, bf16[128,1,512]{2,1,0:T(2,128)(2,1)}, u32[]{:S(2)}) copy-start(bf16[128,1,512]{2,1,0:T(2,128)(2,1)} %copy-done.8) | copy-start | bytes 393220
  116.4 54.0 %copy-start.7 = (bf16[16,8,1536]{2,1,0:T(8,128)(2,1)S(1)}, bf16[16,8,1536]{2,1,0:T(8,128)(2,1)}, u32[]{:S(2)}) copy-start(bf16[16,8,1536]{2,1,0:T(8,128)(2,1)} %constant_dynamic-update-slice_fusion) | copy-start | bytes 1179652
  116.4 54.0 %copy-start.11 = (bf16[16,8,512]{2,1,0:T(8,128)(2,1)S(1)}, bf16[16,8,512]{2,1,0:T(8,128)(2,1)}, u32[]{:S(2)}) copy-start(bf16[16,8,512]{2,1,0:T(8,128)(2,1)} %param.19) | copy-start | bytes 393220
  119.2 147.4 %all-gather.3.cloned.1.call-start = ((), (), s32[]{:S(2)}) async-start(), calls=%async_computation.6 | async-start | bytes 3244032 | tf_op jit(solution)/shard_map/all_gather | solution.py:94
  171.7 15.7 %all-to-all-start.2 = ((bf16[16,8,512]{2,1,0:T(8,128)(2,1)}), bf16[16,8,512]{2,1,0:T(8,128)(2,1)S(1)}, u32[]{:S(2)}, u32[]{:S(2)}) async-start(bf16[16,8,512]{2,1,0:T(8,128)(2,1)} %fusion.17), calls=%async_computation.2 | async-start | bytes 262144 | tf_op jit(solution)/shard_map/all_to_all | solution.py:98
  224.3 11.4 %copy-start.2 = (f32[384,512]{1,0:T(8,128)}, f32[384,512]{1,0:T(8,128)S(1)}, u32[]{:S(2)}) copy-start(f32[384,512]{1,0:T(8,128)S(1)} %scatter_custom_fusion) | copy-start | bytes 2359300
  225.4 33.0 %all-to-all-start.3 = ((bf16[32,8,1024]{2,1,0:T(8,128)(2,1)}), bf16[32,8,1024]{2,1,0:T(8,128)(2,1)}, u32[]{:S(2)}, u32[]{:S(2)}) async-start(bf16[32,8,1024]{2,1,0:T(8,128)(2,1)} %maximum_bitcast_fusion), calls=%async_computation.3 | async-start | bytes 1048576 | tf_op jit(solution)/shard_map/all_to_all | solution.py:113
  235.7 28.7 %copy-start.1 = (bf16[512,1536]{1,0:T(8,128)(2,1)S(1)}, bf16[512,1536]{1,0:T(8,128)(2,1)}, u32[]{:S(2)}) copy-start(bf16[512,1536]{1,0:T(8,128)(2,1)} %param.11) | copy-start | bytes 4718596
Sparse Core Ops, SparseCore 0:
  119.4 50.9 reduce-scatter.1
  173.5 91.0 all-gather.2
